TPU v7x, 32 devices: a whole 2x2x4 slice. The times are simulated.
32 devices in a mesh: row: 8 (over z, y), col: 4 (over x, core).
Axes of the slice: x: 2, y: 2, z: 4, core: 2. Of those that a mesh axis runs over, the one named last changes fastest.
Arguments:
- coeffs: bfloat16 [4096, 1024], P(('row', 'col')), may hold values from -0.1875 to 0.1875
- h_blocks: bfloat16 [8, 4, 8, 4, 128, 128], P('row', 'col'), may hold values from -18 to 18
- block_codes: int32 [8, 4, 8, 4], P('row', 'col'), may hold values from 0 to 4, as said below
Outputs:
- gram: float32 [1024, 1024], P('row', 'col')
Inputs may be any that keep to these rules, and one draw needn't show every extreme that they name: The value 4 * 1 marks an empty slot; the other values within one sub-panel block_codes[r, c, p, :] are distinct. Every tile [r, c] has a sub-panel with no empty slot.
All inputs are finite; a program needn't handle non-finite values.
Results may differ from a plain program's by a relative error of at most 0.0003.
Values may be sent and summed in bfloat16 or wider, within the bound.
A program may use at most 128 MiB of HBM per device.

v0:
```python
import jax
import jax.numpy as jnp
from jax import lax
from jax.sharding import PartitionSpec as P

BLK = 128
CAP = 4
PANEL_BLOCKS = 1


def shards(coeffs, h_blocks, block_codes):
    rows_here = coeffs.shape[0]
    orbital_width = coeffs.shape[1]
    row_count = lax.axis_size("row")
    col_count = lax.axis_size("col")
    tile_brows = rows_here * col_count // BLK
    blocks = h_blocks.reshape(row_count, CAP, BLK, BLK)
    block_code = block_codes.reshape(row_count, CAP)
    block_row = block_code // PANEL_BLOCKS
    panel_pick = block_code % PANEL_BLOCKS
    row_hit = (
        block_row[:, :, None] == jnp.arange(tile_brows, dtype=jnp.int32)[None, None, :]
    ).astype(jnp.bfloat16)
    pick_hit = (
        panel_pick[:, :, None] == jnp.arange(PANEL_BLOCKS, dtype=jnp.int32)[None, None, :]
    ).astype(jnp.bfloat16)
    placement = jnp.einsum(
        "psb,psq->psbq", row_hit, pick_hit, preferred_element_type=jnp.float32
    ).astype(jnp.bfloat16)
    dense_tile = jnp.einsum(
        "psbq,psij->bipqj", placement, blocks, preferred_element_type=jnp.float32
    ).astype(jnp.bfloat16)
    dense_tile = dense_tile.reshape(tile_brows * BLK, row_count * rows_here)
    partial_value = jnp.dot(
        dense_tile,
        lax.all_gather(coeffs, "row", axis=0, tiled=True),
        preferred_element_type=jnp.float32,
    )
    applied = lax.psum_scatter(partial_value, "col", scatter_dimension=0, tiled=True)
    row_width = orbital_width // row_count
    col_width = orbital_width // col_count
    left_split = coeffs.astype(jnp.float32).reshape(coeffs.shape[0], row_count, row_width)
    right_split = applied.reshape(applied.shape[0], col_count, col_width)
    gram_terms = jnp.einsum(
        "nri,ncj->rcij", left_split, right_split, precision=lax.Precision.HIGHEST
    )
    by_col = lax.psum_scatter(gram_terms, "col", scatter_dimension=1, tiled=True)
    gram_tile = lax.psum_scatter(by_col, "row", scatter_dimension=0, tiled=True)
    return gram_tile.reshape(row_width, col_width)


def solution(mesh):
    return jax.shard_map(
        shards,
        mesh=mesh,
        in_specs=(
            P(("row", "col"), None),
            P("row", "col", None, None, None, None),
            P("row", "col", None, None),
        ),
        out_specs=P("row", "col"),
        check_vma=False,
    )
```

profile of v0, /device:TPU:0, one launch (start us, length us, event | category | flops | bytes accessed | tf_op | source)
XLA Modules:
  0.0 220.7 jit_solution(9219067151155303989)
XLA Ops:
  6.5 0.0 copy-start
  6.5 0.0 all-gather.2.cloned.1.call-start
  6.5 0.7 all-gather.2.cloned.1.call-update
  7.3 0.0 reduce-scatter.4.cloned.1.call-start
  7.3 0.8 copy.9
  8.1 0.0 copy-done
  8.1 0.9 fusion
  9.0 0.7 copy.11
  9.7 51.6 %all-gather.2.cloned.1.call-done = bf16[1024,1024]{1,0:T(8,128)(2,1)} async-done(((bf16[128,1024]{1,0:T(8,128)(2,1)}), bf16[1024,1024]{1,0:T(8,128)(2,1)}) %all-gather.2.cloned.1.call-update) | async-done | bytes 2097168 | tf_op jit(solution)/shard_map/all_gather | solution.py:36
  61.3 4.2 %fusion.1 = f32[512,1024]{1,0:T(8,128)} fusion(bf16[1024,1024]{1,0:T(8,128)(2,1)} %all-gather.2.cloned.1.call-done, bf16[64,8,8,128]{3,2,1,0:T(8,128)(2,1)S(1)} %bitcast.41), kind=kOutput, calls=%fused_computation.3 | convolution fusion | flops 1073741824 | bytes 5242880 | tf_op jit(solution)/shard_map/dot_general | solution.py:34
  65.5 0.0 copy-start.1
  65.5 0.0 reduce-scatter.4.cloned.1.call-update
  65.5 0.0 reduce-scatter.6.cloned.1.call-start
  65.6 29.8 %reduce-scatter.4.cloned.1.call-done = f32[128,1024]{1,0:T(8,128)} async-done(((f32[512,1024]{1,0:T(8,128)}), f32[128,1024]{1,0:T(8,128)}) %reduce-scatter.4.cloned.1.call-update) | async-done | bytes 524304 | tf_op jit(solution)/shard_map/reduce_scatter | solution.py:39
  95.3 1.2 copy.17
  96.6 0.0 copy-done.1
  96.6 3.7 %convolution_bitcast_fusion = f32[8,4,128,256]{2,3,0,1:T(8,128)} fusion(f32[128,4,256,1]{0,2,3,1:T(8,128)S(1)} %bitcast.40, bf16[128,1024]{1,0:T(8,128)(2,1)S(1)} %copy-done.1), kind=kOutput, calls=%fused_computation | convolution fusion | flops 1610612736 | bytes 4980736 | tf_op jit(solution)/shard_map/nri,ncj->rcij/dot_general | solution.py:44
  100.3 0.0 reduce-scatter.6.cloned.1.call-update
  100.3 0.0 reduce-scatter.8.cloned.1.call-start
  100.4 44.7 %reduce-scatter.6.cloned.1.call-done = f32[8,1,128,256]{2,3,0,1:T(8,128)} async-done(((f32[8,4,128,256]{2,3,0,1:T(8,128)}), f32[8,1,128,256]{2,3,0,1:T(8,128)}) %reduce-scatter.6.cloned.1.call-update) | async-done | bytes 1048592 | tf_op jit(solution)/shard_map/reduce_scatter | solution.py:47
  145.1 0.0 reduce-scatter.8.cloned.1.call-update
  145.1 67.4 %reduce-scatter.8.cloned.1.call-done = f32[1,1,128,256]{2,3,0,1:T(8,128)} async-done(((f32[8,1,128,256]{2,3,0,1:T(8,128)}), f32[1,1,128,256]{2,3,0,1:T(8,128)}) %reduce-scatter.8.cloned.1.call-update) | async-done | bytes 131088 | tf_op jit(solution)/shard_map/reduce_scatter | solution.py:48
  212.5 1.7 copy.14
Async XLA Ops:
  6.5 1.5 copy-start
  6.5 54.8 %all-gather.2.cloned.1.call-start = ((), (), s32[]{:S(2)}) async-start(), calls=%async_computation.3 | async-start | bytes 2359296 | tf_op jit(solution)/shard_map/all_gather | solution.py:36
  7.3 88.1 %reduce-scatter.4.cloned.1.call-start = ((), (), s32[]{:S(2)}) async-start(), calls=%async_computation.4 | async-start | bytes 2621440 | tf_op jit(solution)/shard_map/reduce_scatter | solution.py:39
  65.5 31.1 %copy-start.1 = (bf16[128,1024]{1,0:T(8,128)(2,1)S(1)}, bf16[128,1024]{1,0:T(8,128)(2,1)}, u32[]{:S(2)}) copy-start(bf16[128,1024]{1,0:T(8,128)(2,1)} %param.3) | copy-start | bytes 786436
  65.5 79.6 %reduce-scatter.6.cloned.1.call-start = ((), (), s32[]{:S(2)}) async-start(), calls=%async_computation.5 | async-start | bytes 5242880 | tf_op jit(solution)/shard_map/reduce_scatter | solution.py:47
  100.3 112.2 %reduce-scatter.8.cloned.1.call-start = ((), (), s32[]{:S(2)}) async-start(), calls=%async_computation.6 | async-start | bytes 1179648 | tf_op jit(solution)/shard_map/reduce_scatter | solution.py:48
Sparse Core Ops, SparseCore 0:
  9.5 51.7 all-gather.1
  65.6 29.6 reduce-scatter.3
  100.4 44.5 reduce-scatter.5
  148.3 64.1 reduce-scatter.7
where the time goes:
time: 221 us
  waiting for transfers between devices  194 us (88%)
  between operations  13.2 us (6%)
  matrix products  8.8 us (4%)
  local copies, waits for them, and re-layouts  4.33 us (2%)
    reduce_scatter x1, waiting for transfers between devices, shards(): gram_tile = lax.psum_scatter(by_col, 'row', scatter_dimension=0, tiled=True)  67.4 us
    all_gather x1, waiting for transfers between devices, shards(): lax.all_gather(coeffs, 'row', axis=0, tiled=True)  51.6 us
    reduce_scatter x1, waiting for transfers between devices, shards(): lax.psum_scatter(gram_terms, 'col', scatter_dimension=1, tiled=True)  44.7 us
    reduce_scatter x1, waiting for transfers between devices, shards(): lax.psum_scatter(partial_value, 'col', scatter_dimension=0, tiled=True)  29.8 us
  transfers between devices with their start and end apart: 4, of which 4 were waited for; matrix products, arithmetic and copies ran while one was open for 1% of the time, Pallas kernels for 0%

commit v1 on v0

v1 whole, which is shorter than its diff:
```python
import functools

import jax
import jax.numpy as jnp
from jax import lax
from jax.experimental import pallas as pl
from jax.experimental.pallas import tpu as pltpu
from jax.sharding import PartitionSpec as P

BLK = 128
CAP = 4
MESH = pl.DeviceIdType.MESH


def ring_order(mesh):
    rows = mesh.shape["row"]
    devices = mesh.devices.reshape(rows, -1)[:, 0]
    try:
        spots = [tuple(int(v) for v in d.coords) for d in devices]
    except (AttributeError, TypeError):
        return list(range(rows))
    axes = [a for a in range(len(spots[0])) if len({s[a] for s in spots}) > 1]
    if len(axes) != 2 or len(set(spots)) != rows:
        return list(range(rows))
    index = {(s[axes[0]], s[axes[1]]): i for i, s in enumerate(spots)}
    first = sorted({s[axes[0]] for s in spots})
    second = sorted({s[axes[1]] for s in spots})
    if len(first) % 2:
        return list(range(rows))
    cycle = []
    for n, a in enumerate(first):
        inner = second[1:] if n % 2 == 0 else second[:0:-1]
        cycle += [(a, b) for b in inner]
    cycle += [(a, second[0]) for a in reversed(first)]
    return [index[key] for key in cycle]


def kernel(order, rc, cc, coeffs, blocks, codes, out,
           cr, hall, codes_all, g, acc, dense, gram, rin,
           local_sem, dir_send, dir_recv, par_send, par_recv,
           own_send, own_recv, ring_send, ring_recv, rs_send, rs_recv):
    r = lax.axis_index("row")
    c = lax.axis_index("col")
    x, k = c // 2, c % 2
    nx = cc // 2
    partner = c + 1 - 2 * k
    half = rc // 2
    width = out.shape[1]
    tall = out.shape[0]
    part = tall // 2
    tb = dense.shape[0] // BLK

    def look(table, i):
        value = jnp.int32(table[0])
        for n in range(1, len(table)):
            value = jnp.where(i == n, jnp.int32(table[n]), value)
        return value

    place = [0] * rc
    for n, row in enumerate(order):
        place[row] = n
    pos = look(place, r)
    behind = [r] + [look(order, lax.rem(pos + rc - s, rc)) for s in range(1, rc)]
    left, right = behind[1], behind[rc - 1]

    def xcol(d, kk):
        return lax.rem(x + nx - d, nx) * 2 + kk

    def cols(i, w):
        return pl.ds(pl.multiple_of(i * w, w), w)

    barrier = pltpu.get_barrier_semaphore()
    friends = [(left, c), (right, c), (r, partner)]
    friends += [(r, xcol(d, k)) for d in range(1, nx)]
    for friend in friends:
        pl.semaphore_signal(barrier, inc=1, device_id=friend, device_id_type=MESH)
    pl.semaphore_wait(barrier, len(friends))

    sent = []

    def send(src, dst, ssem, rsem, device):
        copy = pltpu.make_async_remote_copy(
            src_ref=src, dst_ref=dst, send_sem=ssem, recv_sem=rsem,
            device_id=device, device_id_type=MESH)
        copy.start()
        sent.append(copy)

    def arrived(dst, ssem, rsem, device):
        pltpu.make_async_remote_copy(
            src_ref=dst, dst_ref=dst, send_sem=ssem, recv_sem=rsem,
            device_id=device, device_id_type=MESH).wait_recv()

    def item_ref(source, base_x, n):
        if n < nx:
            return cr.at[source, :, cols(lax.rem(base_x + n, nx), 2 * width)]
        if n == nx:
            return codes_all.at[source]
        return hall.at[source, behind[n - nx - 1]]

    def item_src(base_x, n):
        if n < nx:
            return coeffs.at[:, cols(lax.rem(base_x + n, nx), 2 * width)]
        if n == nx:
            return codes
        return blocks.at[behind[n - nx - 1]]

    def send_item(d, n):
        tx = lax.rem(x + d, nx)
        send(item_src(tx, n), item_ref(c, tx, n), dir_send.at[d - 1, n],
             dir_recv.at[d - 1, n], (r, tx * 2 + k))

    def relay_item(d, n):
        src = item_ref(xcol(d, k), x, n)
        arrived(src, dir_send.at[d - 1, n], dir_recv.at[d - 1, n], (r, xcol(d, k)))
        send(src, src, par_send.at[d - 1, n], par_recv.at[d - 1, n], (r, partner))

    def take_item(d, n):
        dst = item_ref(xcol(d, 1 - k), x, n)
        arrived(dst, par_send.at[d - 1, n], par_recv.at[d - 1, n], (r, partner))

    def moves(step, j, way):
        if step < 1 or step > half:
            return False
        if step == half and rc % 2 == 0:
            return (j % 2) == way
        return True

    def slot(step, way):
        return step if way == 0 else rc - step

    def chunk_col(j):
        return xcol(j // 2, k if j % 2 == 0 else 1 - k)

    def ring_send_to(src, step, j, way):
        send(src, g.at[slot(step, way), chunk_col(j)], ring_send.at[way, step - 1, j],
             ring_recv.at[way, step - 1, j], (right if way == 0 else left, c))

    def ring_first(src, j):
        for way in range(2):
            if moves(1, j, way):
                ring_send_to(src, 1, j, way)

    copies = [
        pltpu.make_async_copy(coeffs, cr.at[c], local_sem.at[0]),
        pltpu.make_async_copy(blocks, hall.at[c], local_sem.at[1]),
        pltpu.make_async_copy(codes, codes_all.at[c], local_sem.at[2]),
    ]
    ring_first(coeffs.at[:, cols(c, width)], 0)
    for d in range(1, nx):
        send_item(d, 0)
    own = [(coeffs, cr.at[c], cr.at[partner]), (codes, codes_all.at[c], codes_all.at[partner]),
           (blocks, hall.at[c], hall.at[partner])]
    for n, (src, dst, _) in enumerate(own):
        send(src, dst, own_send.at[n], own_recv.at[n], (r, partner))
    for copy in copies:
        copy.start()
    hblock = nx + 1
    last_block = hblock + half
    for d in range(1, nx):
        send_item(d, nx)
    sequence = [0]
    for s in range(1, half):
        sequence += [s, rc - s]
    for s in sequence:
        for d in range(1, nx):
            send_item(d, hblock + s)
    for n in range(1, nx):
        for d in range(1, nx):
            send_item(d, n)
    for d in range(1, nx):
        send_item(d, last_block)

    def own_arrived(n):
        arrived(own[n][2], own_send.at[n], own_recv.at[n], (r, partner))

    own_arrived(0)
    ring_first(cr.at[partner, :, cols(c, width)], 1)
    for d in range(1, nx):
        relay_item(d, 0)
        ring_first(cr.at[xcol(d, k), :, cols(c, width)], 2 * d)
        take_item(d, 0)
        ring_first(cr.at[xcol(d, 1 - k), :, cols(c, width)], 2 * d + 1)
    for d in range(1, nx):
        relay_item(d, nx)
    for copy in copies:
        copy.wait()
    own_arrived(1)
    own_arrived(2)
    for d in range(1, nx):
        take_item(d, nx)

    acc[...] = jnp.zeros_like(acc)

    def accumulate(s, xx):
        p = behind[s]
        for kk in range(2):
            tile = xx * 2 + kk
            code = codes_all[tile, pl.ds(p, 1), :]
            block = [hall[tile, p, t] for t in range(CAP)]
            for b in range(tb):
                hit = jnp.where(code == b, 1.0, 0.0).astype(jnp.float32)
                total = None
                for t in range(CAP):
                    pick = jnp.broadcast_to(hit[:, t:t + 1], (1, BLK)).astype(jnp.bfloat16)
                    term = block[t] * pick
                    total = term if total is None else total + term
                dense[pl.ds(b * BLK, BLK), pl.ds(kk * BLK, BLK)] = total
        if s == 0:
            rows = cr[pl.ds(xx * 2, 2), :, cols(c, width)]
        else:
            rows = g[s, pl.ds(xx * 2, 2)]
        acc[...] += jnp.dot(dense[...], rows.reshape(2 * BLK, width),
                            preferred_element_type=jnp.float32)

    def at_distance(s):
        if s == 0 or (2 * s == rc):
            return [s]
        return [s, rc - s]

    accumulate(0, x)
    for step in range(1, half + 1):
        for j in range(cc):
            for way in range(2):
                if moves(step, j, way):
                    here = g.at[slot(step, way), chunk_col(j)]
                    arrived(here, ring_send.at[way, step - 1, j],
                            ring_recv.at[way, step - 1, j],
                            (left if way == 0 else right, c))
                    if moves(step + 1, j, way):
                        ring_send_to(here, step + 1, j, way)
        for s in at_distance(step - 1):
            for d in range(1, nx):
                relay_item(d, hblock + s)
        for s in at_distance(step):
            accumulate(s, x)
        for s in at_distance(step - 1):
            for d in range(1, nx):
                take_item(d, hblock + s)
                accumulate(s, lax.rem(x + nx - d, nx))
    for n in range(1, nx):
        for d in range(1, nx):
            relay_item(d, n)
    for n in range(1, nx):
        for d in range(1, nx):
            take_item(d, n)
    for d in range(1, nx):
        relay_item(d, last_block)
    for d in range(1, nx):
        take_item(d, last_block)
        accumulate(half, lax.rem(x + nx - d, nx))

    applied = acc[...]
    high = applied.astype(jnp.bfloat16)
    low = (applied - high.astype(jnp.float32)).astype(jnp.bfloat16)
    contract = (((0,), (0,)), ((), ()))
    orbitals = coeffs.shape[1]
    step_cols = min(256, orbitals)
    for i in range(orbitals // step_cols):
        lhs = cr[:, :, pl.ds(i * step_cols, step_cols)].reshape(cc * coeffs.shape[0], step_cols)
        gram[pl.ds(i * step_cols, step_cols), :] = (
            lax.dot_general(lhs, high, contract, preferred_element_type=jnp.float32)
            + lax.dot_general(lhs, low, contract, preferred_element_type=jnp.float32))

    def terms(row, piece):
        return pl.ds(pl.multiple_of(row * tall + piece * part, part), part)

    for step in range(1, half + 1):
        for piece in range(2):
            for way in range(2):
                if step == 1 and piece != way:
                    continue
                far = half - step + 1
                dest = behind[rc - far] if way == 0 else behind[far]
                if step == 1 or (step == 2 and piece != way):
                    src = gram.at[terms(dest, piece)]
                else:
                    src = rin.at[way, step - 2, piece]
                    arrived(src, rs_send.at[way, step - 2, piece],
                            rs_recv.at[way, step - 2, piece],
                            (left if way == 0 else right, c))
                    src[...] += gram[terms(dest, piece), :]
                send(src, rin.at[way, step - 1, piece], rs_send.at[way, step - 1, piece],
                     rs_recv.at[way, step - 1, piece], (right if way == 0 else left, c))
    for piece in range(2):
        for way in range(2):
            dst = rin.at[way, half - 1, piece]
            arrived(dst, rs_send.at[way, half - 1, piece], rs_recv.at[way, half - 1, piece],
                    (left if way == 0 else right, c))
        out[pl.ds(piece * part, part), :] = (
            gram[terms(r, piece), :] + rin[0, half - 1, piece] + rin[1, half - 1, piece])
    for copy in sent:
        copy.wait_send()


def shards(order, coeffs, h_blocks, block_codes):
    rc = lax.axis_size("row")
    cc = lax.axis_size("col")
    rows_here, orbitals = coeffs.shape
    tb = rows_here * cc // BLK
    nx = cc // 2
    half = rc // 2
    tall, width = orbitals // rc, orbitals // cc
    blocks = h_blocks.reshape(rc, CAP, BLK, BLK)
    codes = block_codes.reshape(rc, CAP)
    items = nx + 1 + rc
    dma = pltpu.SemaphoreType.DMA
    vmem = pl.BlockSpec(memory_space=pltpu.VMEM)
    peers = max(nx - 1, 1)
    return pl.pallas_call(
        functools.partial(kernel, order, rc, cc),
        out_shape=jax.ShapeDtypeStruct((tall, width), jnp.float32),
        in_specs=[vmem] * 3,
        out_specs=vmem,
        scratch_shapes=[
            pltpu.VMEM((cc, rows_here, orbitals), jnp.bfloat16),
            pltpu.VMEM((cc, rc, CAP, BLK, BLK), jnp.bfloat16),
            pltpu.VMEM((cc, rc, CAP), jnp.int32),
            pltpu.VMEM((rc, cc, rows_here, width), jnp.bfloat16),
            pltpu.VMEM((tb * BLK, width), jnp.float32),
            pltpu.VMEM((tb * BLK, 2 * BLK), jnp.bfloat16),
            pltpu.VMEM((orbitals, width), jnp.float32),
            pltpu.VMEM((2, half, 2, tall // 2, width), jnp.float32),
            dma((3,)),
            dma((peers, items)), dma((peers, items)),
            dma((peers, items)), dma((peers, items)),
            dma((3,)), dma((3,)),
            dma((2, half, cc)), dma((2, half, cc)),
            dma((2, half, 2)), dma((2, half, 2)),
        ],
        compiler_params=pltpu.CompilerParams(
            collective_id=0, has_side_effects=True, vmem_limit_bytes=63 * 1024 * 1024),
    )(coeffs, blocks, codes)


def solution(mesh):
    return jax.shard_map(
        functools.partial(shards, ring_order(mesh)),
        mesh=mesh,
        in_specs=(
            P(("row", "col"), None),
            P("row", "col", None, None, None, None),
            P("row", "col", None, None),
        ),
        out_specs=P("row", "col"),
        check_vma=False,
    )
```

time: 221 us -> 59 us (0.27)
  waiting for transfers between devices: 194 us -> 0 us
  Pallas kernels: 0 us -> 55.9 us
  between operations: 13.2 us -> 0.01 us
  matrix products: 8.8 us -> 0 us
    reduce_scatter x3 -> x0, waiting for transfers between devices: 142 us -> none  [the longest x1 67.4 us: shards(): gram_tile = lax.psum_scatter(by_col, 'row', scatter_dimension=0, tiled=True)]
    pallas_call x0 -> x1, Pallas kernels: none -> 55.9 us  [shards(): pl.pallas_call(functools.partial(kernel, order, rc, cc), out_shape=jax.Sh...]
    all_gather x1 -> x0, waiting for transfers between devices: 51.6 us -> none  [shards(): lax.all_gather(coeffs, 'row', axis=0, tiled=True)]
    dot_general x3 -> x0, matrix products: 8.8 us -> none  [the longest x1 4.18 us: shards(): jnp.dot(dense_tile, lax.all_gather(coeffs, 'row', axis=0, tiled=True), pr...]
    unnamed x4 -> x3, local copies, waits for them, and re-layouts: 0.01 us -> 2.25 us
    reshape x2 -> x1, local copies, waits for them, and re-layouts: 2.89 us -> 0.67 us  [shards(): codes = block_codes.reshape(rc, CAP)]
  transfers between devices with their start and end apart: 4 -> 0, of which waited for: 4 -> 0; matrix products, arithmetic and copies ran while one was open for 1% -> 0% of each run, Pallas kernels for 0% -> 0%
where the time goes in v1:
time: 59 us; the launch traced here: 58.8 us
  Pallas kernels  55.9 us (95%)
  local copies, waits for them, and re-layouts  2.92 us (5%)
    pallas_call x1, Pallas kernels, shards(): pl.pallas_call(functools.partial(kernel, order, rc, cc), out_shape=jax.Sh...  55.9 us
    unnamed x3, local copies, waits for them, and re-layouts  2.25 us

profile of v1, /device:TPU:0, one launch (start us, length us, event | category | flops | bytes accessed | tf_op | source)
XLA Modules:
  0.0 58.8 jit_solution(4091258760439993006)
XLA Ops:
  0.0 0.0 copy-start
  0.0 0.7 %copy-done = s32[1,1,8,4]{2,3,1,0:T(4,128)S(1)} copy-done((s32[1,1,8,4]{2,3,1,0:T(4,128)S(1)}, s32[1,1,8,4]{2,3,1,0:T(4,128)}, u32[]{:S(2)}) %copy-start) | copy-done | bytes 152
  0.7 0.7 %copy.4.codes = s32[8,4]{1,0:T(8,128)} copy(s32[8,4]{0,1:T(4,128)S(1)} %bitcast.3) | data formatting | bytes 256 | tf_op jit(solution)/shard_map/reshape | solution.py:304
  1.4 55.9 %shard_map.37 = f32[128,256]{1,0:T(8,128)} custom-call(bf16[128,1024]{1,0:T(8,128)(2,1)} %coeffs.1, bf16[8,4,128,128]{3,2,1,0:T(8,128)(2,1)} %bitcast.2, s32[8,4]{1,0:T(8,128)} %copy.4.codes), custom_call_target="tpu_custom_call" | custom-call | tf_op jit(solution)/shard_map/pallas_call | solution.py:309
  57.2 1.6 %copy.6 = f32[128,256]{1,0:T(8,128)} copy(f32[128,256]{1,0:T(8,128)} %shard_map.37) | data formatting | bytes 262144
Async XLA Ops:
  0.0 0.7 %copy-start = (s32[1,1,8,4]{2,3,1,0:T(4,128)S(1)}, s32[1,1,8,4]{2,3,1,0:T(4,128)}, u32[]{:S(2)}) copy-start(s32[1,1,8,4]{2,3,1,0:T(4,128)} %param.5) | copy-start | bytes 388

commit v2 on v1

--- a/solution.py
+++ b/solution.py
@@ -9,6 +9,7 @@
 
 BLK = 128
 CAP = 4
+RS_PIECES = 4
 MESH = pl.DeviceIdType.MESH
 
 
@@ -47,7 +48,8 @@
     half = rc // 2
     width = out.shape[1]
     tall = out.shape[0]
-    part = tall // 2
+    pieces = rin.shape[2]
+    part = tall // pieces
     tb = dense.shape[0] // BLK
 
     def look(table, i):
@@ -193,15 +195,17 @@
 
     def accumulate(s, xx):
         p = behind[s]
+        lane = lax.broadcasted_iota(jnp.int32, (CAP, rc), 1)
         for kk in range(2):
             tile = xx * 2 + kk
-            code = codes_all[tile, pl.ds(p, 1), :]
+            marks = codes_all[tile]
+            code = jnp.sum(jnp.where(lane == p, marks, 0), axis=1, keepdims=True)
             block = [hall[tile, p, t] for t in range(CAP)]
             for b in range(tb):
                 hit = jnp.where(code == b, 1.0, 0.0).astype(jnp.float32)
                 total = None
                 for t in range(CAP):
-                    pick = jnp.broadcast_to(hit[:, t:t + 1], (1, BLK)).astype(jnp.bfloat16)
+                    pick = jnp.broadcast_to(hit[t:t + 1, :], (1, BLK)).astype(jnp.bfloat16)
                     term = block[t] * pick
                     total = term if total is None else total + term
                 dense[pl.ds(b * BLK, BLK), pl.ds(kk * BLK, BLK)] = total
@@ -253,25 +257,35 @@
     high = applied.astype(jnp.bfloat16)
     low = (applied - high.astype(jnp.float32)).astype(jnp.bfloat16)
     contract = (((0,), (0,)), ((), ()))
-    orbitals = coeffs.shape[1]
-    step_cols = min(256, orbitals)
-    for i in range(orbitals // step_cols):
-        lhs = cr[:, :, pl.ds(i * step_cols, step_cols)].reshape(cc * coeffs.shape[0], step_cols)
-        gram[pl.ds(i * step_cols, step_cols), :] = (
+    blockwise = tall % BLK == 0
+
+    def gram_rows(start, size):
+        lhs = cr[:, :, pl.ds(start, size)].reshape(cc * coeffs.shape[0], size)
+        gram[pl.ds(start, size), :] = (
             lax.dot_general(lhs, high, contract, preferred_element_type=jnp.float32)
             + lax.dot_general(lhs, low, contract, preferred_element_type=jnp.float32))
 
+    def gram_for(row):
+        if blockwise:
+            gram_rows(pl.multiple_of(row * tall, tall), tall)
+
+    if not blockwise:
+        for i in range(coeffs.shape[1] // BLK):
+            gram_rows(i * BLK, BLK)
+
     def terms(row, piece):
         return pl.ds(pl.multiple_of(row * tall + piece * part, part), part)
 
     for step in range(1, half + 1):
-        for piece in range(2):
+        for s in at_distance(half - step + 1):
+            gram_for(behind[s])
+        for piece in range(pieces):
             for way in range(2):
-                if step == 1 and piece != way:
+                if step == 1 and piece % 2 != way:
                     continue
                 far = half - step + 1
                 dest = behind[rc - far] if way == 0 else behind[far]
-                if step == 1 or (step == 2 and piece != way):
+                if step == 1 or (step == 2 and piece % 2 != way):
                     src = gram.at[terms(dest, piece)]
                 else:
                     src = rin.at[way, step - 2, piece]
@@ -281,7 +295,8 @@
                     src[...] += gram[terms(dest, piece), :]
                 send(src, rin.at[way, step - 1, piece], rs_send.at[way, step - 1, piece],
                      rs_recv.at[way, step - 1, piece], (right if way == 0 else left, c))
-    for piece in range(2):
+    gram_for(r)
+    for piece in range(pieces):
         for way in range(2):
             dst = rin.at[way, half - 1, piece]
             arrived(dst, rs_send.at[way, half - 1, piece], rs_recv.at[way, half - 1, piece],
@@ -301,7 +316,7 @@
     half = rc // 2
     tall, width = orbitals // rc, orbitals // cc
     blocks = h_blocks.reshape(rc, CAP, BLK, BLK)
-    codes = block_codes.reshape(rc, CAP)
+    codes = block_codes.reshape(rc, CAP).T
     items = nx + 1 + rc
     dma = pltpu.SemaphoreType.DMA
     vmem = pl.BlockSpec(memory_space=pltpu.VMEM)
@@ -309,23 +324,23 @@
     return pl.pallas_call(
         functools.partial(kernel, order, rc, cc),
         out_shape=jax.ShapeDtypeStruct((tall, width), jnp.float32),
-        in_specs=[vmem] * 3,
+        in_specs=[pl.BlockSpec(memory_space=pl.ANY)] * 3,
         out_specs=vmem,
         scratch_shapes=[
             pltpu.VMEM((cc, rows_here, orbitals), jnp.bfloat16),
             pltpu.VMEM((cc, rc, CAP, BLK, BLK), jnp.bfloat16),
-            pltpu.VMEM((cc, rc, CAP), jnp.int32),
+            pltpu.VMEM((cc, CAP, rc), jnp.int32),
             pltpu.VMEM((rc, cc, rows_here, width), jnp.bfloat16),
             pltpu.VMEM((tb * BLK, width), jnp.float32),
             pltpu.VMEM((tb * BLK, 2 * BLK), jnp.bfloat16),
             pltpu.VMEM((orbitals, width), jnp.float32),
-            pltpu.VMEM((2, half, 2, tall // 2, width), jnp.float32),
+            pltpu.VMEM((2, half, RS_PIECES, tall // RS_PIECES, width), jnp.float32),
             dma((3,)),
             dma((peers, items)), dma((peers, items)),
             dma((peers, items)), dma((peers, items)),
             dma((3,)), dma((3,)),
             dma((2, half, cc)), dma((2, half, cc)),
-            dma((2, half, 2)), dma((2, half, 2)),
+            dma((2, half, RS_PIECES)), dma((2, half, RS_PIECES)),
         ],
         compiler_params=pltpu.CompilerParams(
             collective_id=0, has_side_effects=True, vmem_limit_bytes=63 * 1024 * 1024),

time: 59 us -> 54.3 us (0.920)
  Pallas kernels: 55.9 us -> 52.6 us
  local copies, waits for them, and re-layouts: 2.92 us -> 1.57 us
    pallas_call x1, Pallas kernels: 55.9 us -> 52.6 us  [shards(): pl.pallas_call(functools.partial(kernel, order, rc, cc), out_shape=jax.Sh...]
    unnamed x3 -> x1, local copies, waits for them, and re-layouts: 2.25 us -> 1.57 us
    reshape x1 -> x0, local copies, waits for them, and re-layouts: 0.67 us -> none  [shards(): codes = block_codes.reshape(rc, CAP)]
where the time goes in v2:
time: 54.3 us; the launch traced here: 54.2 us
  Pallas kernels  52.6 us (97%)
  local copies, waits for them, and re-layouts  1.57 us (3%)
    pallas_call x1, Pallas kernels, shards(): pl.pallas_call(functools.partial(kernel, order, rc, cc), out_shape=jax.Sh...  52.6 us
    unnamed x1, local copies, waits for them, and re-layouts  1.57 us

profile of v2, /device:TPU:0, one launch (start us, length us, event | category | flops | bytes accessed | tf_op | source)
XLA Modules:
  0.0 54.2 jit_solution(5424199458641734358)
XLA Ops:
  0.0 52.6 %shard_map.37 = f32[128,256]{1,0:T(8,128)} custom-call(bf16[128,1024]{1,0:T(8,128)(2,1)} %coeffs.1, bf16[8,4,128,128]{3,2,1,0:T(8,128)(2,1)} %bitcast.4, s32[4,8]{1,0:T(4,128)} %bitcast.5), custom_call_target="tpu_custom_call" | custom-call | tf_op jit(solution)/shard_map/pallas_call | solution.py:324
  52.6 1.6 %copy.5 = f32[128,256]{1,0:T(8,128)} copy(f32[128,256]{1,0:T(8,128)} %shard_map.37) | data formatting | bytes 262144
